TPU v7x, 128 devices: a whole 4x4x4 slice. The times are simulated.
128 devices in a mesh: gx: 16 (over y, z), gy: 8 (over x, core).
Axes of the slice: x: 4, y: 4, z: 4, core: 2. Of those that a mesh axis runs over, the one named last changes fastest.
Arguments:
- snapshots: bfloat16 [16, 16, 4, 2048, 512], P('gx', 'gy'), may hold values from -120 to 120
- basis: bfloat16 [16, 16, 4, 24, 2048], P('gx', 'gy'), may hold values from -0.0625 to 0.0625
- node_counts: int32 [16, 16], P('gx', 'gy'), may hold values from 1024 to 2048, as said below
- adjacency: int32 [16, 16, 3], P('gx', 'gy'), may hold values from 0 to 255, as said below
Outputs:
- operator: float32 [16, 16, 397, 24], P('gx', 'gy')
- reduced_states: float32 [16, 16, 24, 512], P('gx', 'gy')
Inputs may be any that keep to these rules, and one draw needn't show every extreme that they name: Node slot n of subdomain g is live iff n < node_counts[g]; at least 1024 slots are live, and one subdomain has all 2048 live. Subdomain (row, col) has id row * 16 + col. Each row of adjacency holds 3 distinct ids other than its own subdomain's, each within one subdomain row and one subdomain column of it.
All inputs are finite; a program needn't handle non-finite values.
Results may differ from a plain program's by a relative error of at most 0.0003.
Values sent between devices are 32-bit elements; how exact they have to be, the bound alone decides.
A program may use at most 64 MiB of HBM per device.

v0:
```python
import jax
import jax.numpy as jnp
from jax import lax
from jax.sharding import Mesh
from jax.sharding import PartitionSpec as P

GX = ("gx_0", "gx_1")
GY = ("gy_0", "gy_1")
GX_GY = ("gx_0", "gx_1", "gy_0", "gy_1")


beta_linear = 0.5
beta_quad = 0.5


def one_axis_at_a_time(x, axes):
    for axis in axes:
        x = lax.psum(x, axis)
    return x


def padded_2(cells, sides, width):
    for axis, dim in sides:
        count = lax.axis_size(axis)
        ends = count - 1
        head = lax.slice_in_dim(cells, 0, width, axis=dim)
        tail = lax.slice_in_dim(cells, cells.shape[dim] - width, cells.shape[dim], axis=dim)
        cells = jnp.concatenate(
            [
                lax.ppermute(tail, axis, [(i, (i + 1) % count) for i in range(ends)]),
                cells,
                lax.ppermute(head, axis, [((i + 1) % count, i) for i in range(ends)]),
            ],
            axis=dim,
        )
    return cells


def build_features(state, near):
    ranks = state.shape[1]
    steps = state.shape[2]
    pieces = [
        jnp.ones((state.shape[0], 1, steps), jnp.float32),
        state,
        near.reshape(state.shape[0], -1, steps),
    ]
    for first in range(ranks):
        pieces.append(state[:, first : first + 1] * state[:, first:])
    return jnp.concatenate(pieces, axis=1)


def pick_rows(pieces, links):
    ids = jnp.arange(pieces.shape[0], dtype=jnp.int32)
    hits = (links[:, :, None] == ids[None, None, :]).astype(jnp.float32)
    return jnp.einsum("sbn,nrk->sbrk", hits, pieces, precision=lax.Precision.HIGHEST)


def solve_one(gram, rhs):
    factor = jnp.linalg.cholesky(gram)
    middle = jax.scipy.linalg.solve_triangular(factor, rhs, lower=True)
    return jax.scipy.linalg.solve_triangular(factor, middle, lower=True, trans=1)


def body(snapshots, basis, node_counts, adjacency):
    values = snapshots[0]
    modes = basis[0]
    counts = node_counts[0]
    links = adjacency[0]
    columns = values.shape[0]
    slots = values.shape[2]
    steps = values.shape[3]
    ranks = modes.shape[2]
    live = jnp.arange(slots, dtype=jnp.int32)[None, :] < counts[:, None]
    masked = modes * live.astype(jnp.bfloat16)[:, None, None, :]
    proj = jnp.einsum("svrp,svpk->svrk", masked, values, preferred_element_type=jnp.float32)
    slotsq = jnp.einsum("svpk,svpk->svp", values, values, preferred_element_type=jnp.float32)
    squares = jnp.sum(slotsq * live.astype(jnp.float32)[:, None, :], axis=(0, 2))
    nodes = jnp.sum(counts.astype(jnp.float32))
    total_subs = lax.axis_size(GX) * lax.axis_size(GY) * columns
    grid_cols = columns * lax.axis_size(GY)
    near_row = links // grid_cols
    near_col = links % grid_cols
    local = (near_row - lax.axis_index(GX) + 1) * (columns + 2) + (
        near_col - lax.axis_index(GY) * columns + 1
    )
    cross = jnp.einsum("svrk,swrk->vw", proj, proj, precision=lax.Precision.HIGHEST)
    sq_all, nodes_all, cross_all = (
        one_axis_at_a_time(squares, GX_GY),
        one_axis_at_a_time(nodes, GX_GY),
        one_axis_at_a_time(cross, GX_GY),
    )
    scale = jnp.sqrt(sq_all / (nodes_all * steps) + 1e-06)
    states = jnp.sum(proj / scale[None, :, None, None], axis=1)
    gnorm = jnp.sum(cross_all / (scale[:, None] * scale[None, :])) / (total_subs * ranks * steps)
    padded = padded_2(states[None], ((GX, 0), (GY, 1)), 1)
    flat = padded.reshape(-1, ranks, steps)
    near = pick_rows(flat, local)
    nbrs = links.shape[1]
    feats = build_features(states, near)
    past = feats[:, :, :-1]
    nlin = 1 + ranks + nbrs * ranks
    nquad = ranks * (ranks + 1) // 2
    reg_diag = steps * jnp.concatenate(
        [
            jnp.full((nlin,), beta_linear, jnp.float32) * gnorm,
            jnp.full((nquad,), beta_quad, jnp.float32) * gnorm * gnorm,
        ]
    )
    gram = (
        jnp.einsum("sfk,sgk->sfg", past, past, precision=lax.Precision.HIGHEST)
        + jnp.diag(reg_diag)[None]
    )
    rhs = jnp.einsum("sfk,srk->sfr", past, states[:, :, 1:], precision=lax.Precision.HIGHEST)
    operator = jax.vmap(solve_one)(gram, rhs)
    return (operator[None], states[None])


def solution(mesh):
    split = Mesh(mesh.devices.reshape(4, 4, 4, 2), ("gx_0", "gx_1", "gy_0", "gy_1"))
    placed = (P(GX, GY, None, None, None), P(GX, GY, None, None, None), P(GX, GY), P(GX, GY, None))
    return jax.shard_map(
        body,
        mesh=split,
        in_specs=placed,
        out_specs=(P(GX, GY, None, None), P(GX, GY, None, None)),
        check_vma=False,
    )
```

profile of v0, /device:TPU:1, one launch (start us, length us, event | category | flops | bytes accessed | tf_op | source)
XLA Modules:
  0.0 333.4 jit_solution(6899208880659183131)
XLA Ops:
  0.6 0.7 fusion.58
  1.4 7.5 %fusion = f32[2,4,2048]{2,1,0:T(4,128)S(1)} fusion(bf16[1,2,4,2048,512]{4,3,2,1,0:T(8,128)(2,1)} %param.4), kind=kLoop, calls=%fused_computation.3 | loop fusion | flops 25149440 | bytes 16842752 | tf_op jit(solution)/shard_map/svpk,svpk->svp/dot_general | solution.py:76
  8.9 3.2 copy-done
  12.0 3.4 %fusion.1 = f32[2,4,24,512]{3,2,1,0:T(8,128)S(1)} fusion(bf16[1,2,4,2048,512]{4,3,2,1,0:T(8,128)(2,1)S(1)} %copy-done, bf16[1,2,4,24,2048]{4,3,2,1,0:T(8,128)(2,1)} %param.5, bf16[2,2048]{1,0:T(2,128)(2,1)S(1)} %get-tuple-element.70), kind=kOutput, calls=%fused_computation.4 | convolution fusion | flops 403046400 | bytes 17965056 | tf_op jit(solution)/shard_map/svrp,svpk->svrk/dot_general | solution.py:75
  15.5 1.9 convolution_bitcast_fusion
  17.5 0.6 convert_reduce_fusion
  18.1 10.1 %all-reduce.6 = (f32[4]{0:T(128)S(1)}, f32[]{:T(128)}, f32[4,4]{1,0:T(4,128)S(1)}) all-reduce(f32[4]{0:T(128)S(1)} %multiply_reduce_fusion, f32[]{:T(128)} %convert_reduce_fusion, f32[4,4]{1,0:T(4,128)S(1)} %convolution_bitcast_fusion), channel_id=1, replica_groups=mesh['gx_0'=4,'gx_1'=4,'gy_0'=4,'gy_1'=2] {'gx_0'}, use_global_device_ids=true, to_apply=%region_1.0 | all-reduce | flops 21 | bytes 168 | tf_op jit(solution)/shard_map/psum | solution.py:18
  28.3 10.4 %all-reduce.5 = (f32[4]{0:T(128)S(1)}, f32[]{:T(128)}, f32[4,4]{1,0:T(4,128)S(1)}) all-reduce(f32[4]{0:T(128)S(1)} %get-tuple-element.27, f32[]{:T(128)} %get-tuple-element.28, f32[4,4]{1,0:T(4,128)S(1)} %get-tuple-element.29), channel_id=1, replica_groups=mesh['gx_0'=4,'gx_1'=4,'gy_0'=4,'gy_1'=2] {'gx_1'}, use_global_device_ids=true, to_apply=%region_2.3 | all-reduce | flops 21 | bytes 168 | tf_op jit(solution)/shard_map/psum | solution.py:18
  38.6 9.1 %all-reduce.4 = (f32[4]{0:T(128)S(1)}, f32[]{:T(128)}, f32[4,4]{1,0:T(4,128)S(1)}) all-reduce(f32[4]{0:T(128)S(1)} %get-tuple-element.24, f32[]{:T(128)} %get-tuple-element.25, f32[4,4]{1,0:T(4,128)S(1)} %get-tuple-element.26), channel_id=1, replica_groups=mesh['gx_0'=4,'gx_1'=4,'gy_0'=4,'gy_1'=2] {'gy_0'}, use_global_device_ids=true, to_apply=%region_3.4 | all-reduce | flops 21 | bytes 168 | tf_op jit(solution)/shard_map/psum | solution.py:18
  47.7 9.5 %all-reduce.7 = (f32[4]{0:T(128)S(1)}, f32[]{:T(128)}, f32[4,4]{1,0:T(4,128)S(1)}) all-reduce(f32[4]{0:T(128)S(1)} %get-tuple-element.21, f32[]{:T(128)} %get-tuple-element.22, f32[4,4]{1,0:T(4,128)S(1)} %get-tuple-element.23), channel_id=1, replica_groups=mesh['gx_0'=4,'gx_1'=4,'gy_0'=4,'gy_1'=2] {'gy_1'}, use_global_device_ids=true, to_apply=%region_4.5 | all-reduce | flops 21 | bytes 168 | tf_op jit(solution)/shard_map/psum | solution.py:18
  58.0 1.3 collective-permute-start.1
  59.3 4.0 %collective-permute-start = (f32[1,2,24,512]{3,2,1,0:T(8,128)S(1)}, f32[1,2,24,512]{3,2,1,0:T(8,128)S(1)}, u32[]{:S(2)}, u32[]{:S(2)}) collective-permute-start(f32[1,2,24,512]{3,2,1,0:T(8,128)S(1)} %bitcast.156), channel_id=1, source_target_pairs={{0,8},{8,16},{16,24},{24,32},{32,40},{40,48},{48,56},{56,64},{64,7... | collective-permute-start | bytes 294920 | tf_op jit(solution)/shard_map/ppermute | solution.py:30
  63.3 0.6 iota_compare_fusion.4
  63.9 0.7 slice_multiply_fusion.22
  64.6 0.6 pad_convert_fusion
  65.2 0.8 fusion.65
  68.1 0.6 slice_multiply_fusion.21
  68.7 0.6 slice_multiply_fusion.20
  69.3 0.6 slice_multiply_fusion.19
  69.9 0.6 slice_multiply_fusion.18
  70.5 0.6 slice_multiply_fusion.16
  71.1 0.6 slice_multiply_fusion.17
  71.8 0.6 slice_multiply_fusion.15
  72.9 1.4 fusion.9
  74.3 0.6 iota_compare_fusion.8
  74.9 2.0 collective-permute-start.2
  77.0 2.5 collective-permute-start.3
  79.4 0.6 iota_multiply_fusion
  80.0 0.8 iota_compare_fusion.2
  80.8 2.7 collective-permute-done.3
  83.5 0.8 fusion.11
  84.3 8.0 %concatenate.48 = f32[2,397,512]{2,1,0:T(8,128)S(1)} concatenate(f32[2,1,512]{2,1,0:T(1,128)S(1)} %broadcast_in_dim.45, f32[2,24,512]{2,1,0:T(8,128)S(1)} %divide_reduce_fusion, f32[2,72,512]{2,1,0:T(8,128)S(1)} %bitcast.161, f32[2,24,512]{2,1,0:T(8,128)S(1)} %broadcast_multiply_fusion, f32[2,23,512]{2,1,0:T(8,128)S(1)} %slice_multiply_fusion.6, ...), dimensions={1} | concatenate | bytes 3252224 | tf_op jit(solution)/shard_map/concatenate | solution.py:49
  92.4 1.5 fusion.5
  93.9 2.8 fusion.7
  96.7 0.7 copy.49
  97.4 2.0 fusion.4
  99.4 1.2 copy-done.2
  100.6 23.5 %custom-call.38 = f32[2,128,128]{2,1,0:T(8,128)S(1)} custom-call(f32[2,128,128]{2,1,0:T(8,128)S(1)} %cholesky.281), custom_call_target="Cholesky" | custom-call | tf_op jit(solution)/shard_map/vmap(jit(cholesky))/cholesky | solution.py:59
  124.1 19.9 %custom-call.39 = f32[2,1,128,128]{2,3,1,0:T(8,128)S(1)} custom-call(f32[2,1,128,128]{3,2,1,0:T(8,128)S(1)} %select_bitcast_fusion.2), custom_call_target="InvertDiagBlocksLowerTriangular" | custom-call | tf_op jit(solution)/shard_map/vmap(jit(cholesky))/cholesky | solution.py:59
  144.2 1.4 constant_dynamic-update-slice_fusion.3
  145.6 1.4 convolution_subtract_fusion
  147.0 23.5 %custom-call.40 = f32[2,128,128]{2,1,0:T(8,128)S(1)} custom-call(f32[2,128,128]{2,1,0:T(8,128)S(1)} %cholesky.285), custom_call_target="Cholesky" | custom-call | tf_op jit(solution)/shard_map/vmap(jit(cholesky))/cholesky | solution.py:59
  170.5 19.7 %custom-call.41 = f32[2,1,128,128]{2,3,1,0:T(8,128)S(1)} custom-call(f32[2,1,128,128]{3,2,1,0:T(8,128)S(1)} %get-tuple-element.39), custom_call_target="InvertDiagBlocksLowerTriangular" | custom-call | tf_op jit(solution)/shard_map/vmap(jit(cholesky))/cholesky | solution.py:59
  190.5 1.3 convolution_subtract_fusion.1
  191.8 23.7 %custom-call.42 = f32[2,128,128]{2,1,0:T(8,128)S(1)} custom-call(f32[2,128,128]{2,1,0:T(8,128)S(1)} %cholesky.290), custom_call_target="Cholesky" | custom-call | tf_op jit(solution)/shard_map/vmap(jit(cholesky))/cholesky | solution.py:59
  215.9 19.7 %custom-call.43 = f32[2,1,128,128]{2,3,1,0:T(8,128)S(1)} custom-call(f32[2,1,128,128]{3,2,1,0:T(8,128)S(1)} %get-tuple-element.37), custom_call_target="InvertDiagBlocksLowerTriangular" | custom-call | tf_op jit(solution)/shard_map/vmap(jit(cholesky))/cholesky | solution.py:59
  235.9 0.9 convolution_subtract_fusion.8
  236.8 2.4 custom-call.44
  239.3 1.3 select_select_fusion
  240.7 7.9 %while.1 = (s32[]{:T(128)}, f32[2,397,397]{2,1,0:T(8,128)S(1)}, s32[3,2]{0,1:T(2,128)S(1)}, f32[3,2,128,128]{3,2,0,1:T(8,128)}, s32[]{:T(128)}) while((s32[]{:T(128)}, f32[2,397,397]{2,1,0:T(8,128)S(1)}, s32[3,2]{0,1:T(2,128)S(1)}, f32[3,2,128,128]{3,2,0,1:T(8,128)}, s32[]{:T(128)}) %tuple.67), condition=%wide.while_cond, body=%wide.while_body.sunk | while | flops 2 | bytes 263277 | solution.py:61
  240.7 0.6 fusion.85
  241.3 2.0 bitcast_dynamic-update-slice_fusion.2
  243.4 0.6 fusion.85
  244.0 2.0 bitcast_dynamic-update-slice_fusion.2
  246.0 0.6 fusion.85
  246.6 2.0 bitcast_dynamic-update-slice_fusion.2
  248.7 1.0 pad_maximum_fusion.1
  249.7 78.6 %custom-call.45 = f32[2,4,128,128]{2,3,1,0:T(8,128)S(1)} custom-call(f32[2,4,128,128]{3,2,1,0:T(8,128)S(1)} %pad_maximum_fusion.1), custom_call_target="InvertDiagBlocksLowerTriangular" | custom-call | tf_op jit(solution)/shard_map/vmap(jit(_solve_triangular))/triangular_solve | solution.py:61
  328.6 0.3 convolution_subtract_fusion.6
  329.2 0.3 convolution_subtract_fusion.5
  331.3 0.3 fusion.32
  331.6 0.3 convolution_subtract_fusion.7
  331.9 0.3 fusion.30
  332.3 0.7 maximum_bitcast_fusion
  (93 shorter events, 4.8 us)
Async XLA Ops:
  1.4 10.7 %copy-start = (bf16[1,2,4,2048,512]{4,3,2,1,0:T(8,128)(2,1)S(1)}, bf16[1,2,4,2048,512]{4,3,2,1,0:T(8,128)(2,1)}, u32[]{:S(2)}) copy-start(bf16[1,2,4,2048,512]{4,3,2,1,0:T(8,128)(2,1)} %param.4) | copy-start | bytes 50331652
  12.0 5.5 %copy-start.7 = (s32[1,2]{1,0:T(1,128)S(1)}, s32[1,2]{1,0:T(1,128)}, u32[]{:S(2)}) copy-start(s32[1,2]{1,0:T(1,128)} %param.6) | copy-start | bytes 28
  58.0 34.4 %copy-start.1 = (f32[2,24,512]{2,1,0:T(8,128)}, f32[2,24,512]{2,1,0:T(8,128)S(1)}, u32[]{:S(2)}) copy-start(f32[2,24,512]{2,1,0:T(8,128)S(1)} %divide_reduce_fusion) | copy-start | bytes 294916
  58.0 16.9 %collective-permute-start.1 = (f32[1,2,24,512]{3,2,1,0:T(8,128)S(1)}, f32[1,2,24,512]{3,2,1,0:T(8,128)S(1)}, u32[]{:S(2)}, u32[]{:S(2)}) collective-permute-start(f32[1,2,24,512]{3,2,1,0:T(8,128)S(1)} %bitcast.155), channel_id=1, source_target_pairs={{8,0},{16,8},{24,16},{32,24},{40,32},{48,40},{56,48},{64,56},{72,6... | collective-permute-start | bytes 294920 | tf_op jit(solution)/shard_map/ppermute | solution.py:32
  59.3 15.6 %collective-permute-start = (f32[1,2,24,512]{3,2,1,0:T(8,128)S(1)}, f32[1,2,24,512]{3,2,1,0:T(8,128)S(1)}, u32[]{:S(2)}, u32[]{:S(2)}) collective-permute-start(f32[1,2,24,512]{3,2,1,0:T(8,128)S(1)} %bitcast.156), channel_id=1, source_target_pairs={{0,8},{8,16},{16,24},{24,32},{32,40},{40,48},{48,56},{56,64},{64,7... | collective-permute-start | bytes 294920 | tf_op jit(solution)/shard_map/ppermute | solution.py:30
  72.6 1.7 copy-start.6
  74.9 5.8 %collective-permute-start.2 = (f32[3,1,24,512]{3,2,1,0:T(8,128)S(1)}, f32[3,1,24,512]{3,2,1,0:T(8,128)S(1)}, u32[]{:S(2)}, u32[]{:S(2)}) collective-permute-start(f32[3,1,24,512]{3,2,1,0:T(8,128)S(1)} %get-tuple-element.35), channel_id=1, source_target_pairs={{0,1},{1,2},{2,3},{3,4},{4,5},{5,6},{6,7},{8,9},{9,10},{10,11},{11... | collective-permute-start | bytes 442376 | tf_op jit(solution)/shard_map/ppermute | solution.py:30
  77.0 6.5 %collective-permute-start.3 = (f32[3,1,24,512]{3,2,1,0:T(8,128)S(1)}, f32[3,1,24,512]{3,2,1,0:T(8,128)S(1)}, u32[]{:S(2)}, u32[]{:S(2)}) collective-permute-start(f32[3,1,24,512]{3,2,1,0:T(8,128)S(1)} %get-tuple-element.36), channel_id=1, source_target_pairs={{1,0},{2,1},{3,2},{4,3},{5,4},{6,5},{7,6},{9,8},{10,9},{11,10},{12... | collective-permute-start | bytes 442376 | tf_op jit(solution)/shard_map/ppermute | solution.py:32
  99.4 1.2 copy-start.2
  145.6 69.9 %copy-start.4 = (pred[128,128]{1,0:T(8,128)(4,1)S(1)}, pred[128,128]{1,0:T(8,128)(4,1)}, u32[]{:S(2)}) copy-start(pred[128,128]{1,0:T(8,128)(4,1)} %get-tuple-element.96) | copy-start | bytes 49156
  147.0 92.2 %copy-start.5 = (pred[13,13]{1,0:T(8,128)(4,1)S(1)}, pred[13,13]{1,0:T(8,128)(4,1)}, u32[]{:S(2)}) copy-start(pred[13,13]{1,0:T(8,128)(4,1)} %iota_compare_fusion.8) | copy-start | bytes 511
  239.3 1.3 copy-start.8
  239.3 9.2 %copy-start.3 = (f32[128,115]{1,0:T(8,128)S(1)}, f32[128,115]{1,0:T(8,128)}, u32[]{:S(2)}) copy-start(f32[128,115]{1,0:T(8,128)} %pad_convert_fusion) | copy-start | bytes 176644
where the time goes:
time: 338 us; the launch traced here: 333 us
  other arithmetic  236 us (70%)
  blocking collectives  39 us (12%)
  local copies, waits for them, and re-layouts  21.6 us (6%)
  matrix products  19.6 us (6%)
  starting transfers between devices  9.79 us (3%)
  between operations  4.41 us (1%)
    another operation x18, other arithmetic, solve_one(): factor = jnp.linalg.cholesky(gram)  134 us
    another operation x8, other arithmetic, solve_one(): jax.scipy.linalg.solve_triangular(factor, middle, lower=True, trans=1)  83 us
    psum x4, blocking collectives, one_axis_at_a_time(): x = lax.psum(x, axis)  39 us
    concatenate x1, local copies, waits for them, and re-layouts, build_features(): return jnp.concatenate(pieces, axis=1)  8.01 us
    another operation x9, local copies, waits for them, and re-layouts  7.89 us
    dot_general x1, other arithmetic, body(): jnp.einsum('svpk,svpk->svp', values, values, preferred_element_type=jnp.f...  7.47 us
  transfers between devices with their start and end apart: 4, of which 1 were waited for; matrix products, arithmetic and copies ran while one was open for 3% of the time, Pallas kernels for 0%

commit v1 on v0

v1 whole, which is shorter than its diff:
```python
import functools

import jax
import jax.numpy as jnp
from jax import lax
from jax.experimental import pallas as pl
from jax.experimental.pallas import tpu as pltpu
from jax.sharding import PartitionSpec as P

MESH = pl.DeviceIdType.MESH
F32 = jnp.float32
BF16 = jnp.bfloat16
R = 24
NV = 4
PAIRS = [(v, w) for v in range(NV) for w in range(v, NV)]
ROWS = 400
QUAD_END = 300
OWN = 304
NEAR = 328
HALF = 64


def feature_rows():
    place = {}
    for a in range(3):
        for r in range(4):
            for m in range(8):
                i, j = 8 * a + m, 8 * a + (m + r) % 8
                place[(min(i, j), max(i, j))] = (4 * a + r) * 8 + m
    for c, (a, b) in enumerate(((0, 1), (0, 2), (1, 2))):
        for r in range(8):
            for m in range(8):
                place[(8 * a + m, 8 * b + (m + r) % 8)] = (12 + 8 * c + r) * 8 + m
    for m in range(4):
        place[(m, m + 4)] = 288 + m
        place[(8 + m, 12 + m)] = 292 + m
        place[(16 + m, 20 + m)] = 296 + m
    rows = [QUAD_END] + list(range(OWN, OWN + R)) + list(range(NEAR, NEAR + 3 * R))
    for i in range(R):
        for j in range(i, R):
            rows.append(place[(i, j)])
    return rows


SOURCE = feature_rows()


def iota(shape, dim):
    return lax.broadcasted_iota(jnp.int32, shape, dim)


def split2(x):
    hi = x.astype(BF16)
    return hi, (x - hi.astype(F32)).astype(BF16)


def mm(a, b):
    return jnp.dot(a, b, preferred_element_type=F32)


def mm_nt(a, b):
    return lax.dot_general(a, b, (((1,), (1,)), ((), ())), preferred_element_type=F32)


def scan_kernel(counts_ref, vals_ref, modes_ref, proj_ref, stats_ref, acc_ref):
    s = pl.program_id(0)
    v = pl.program_id(1)
    count = counts_ref[0, s]
    slots = vals_ref.shape[0]

    @pl.when((s == 0) & (v == 0))
    def _():
        acc_ref[...] = jnp.zeros_like(acc_ref)

    lanes = iota((R, slots), 1)
    modes = jnp.where(lanes < count, modes_ref[...].astype(F32), 0.0).astype(BF16)
    proj_ref[pl.ds(v, 1)] = mm(modes, vals_ref[...])[None]
    chunk = 128

    def step(c, acc):
        x = vals_ref[pl.ds(pl.multiple_of(c * chunk, chunk), chunk), :].astype(F32)
        rows = iota((chunk, x.shape[1]), 0) + c * chunk
        x = jnp.where(rows < count, x, 0.0)
        x = x * x
        x = jnp.sum(x.reshape(chunk // 8, 8, x.shape[1]), axis=0)
        return acc + x

    sq = lax.fori_loop(0, slots // chunk, step, jnp.zeros((8, vals_ref.shape[1]), F32))
    sq = sq[:, 0:128] + sq[:, 128:256] + sq[:, 256:384] + sq[:, 384:512]
    acc_ref[pl.ds(v, 1)] += sq[None]

    @pl.when(v == NV - 1)
    def _():
        for n, (a, b) in enumerate(PAIRS):
            x = proj_ref[a] * proj_ref[b]
            x = x[0:8] + x[8:16] + x[16:24]
            acc_ref[NV + n] += x[:, 0:128] + x[:, 128:256] + x[:, 256:384] + x[:, 384:512]

    @pl.when((s == 1) & (v == NV - 1))
    def _():
        rows = [jnp.sum(acc_ref[n], axis=0, keepdims=True) for n in range(NV + len(PAIRS))]
        rows += [jnp.zeros((1, 128), F32)] * (16 - len(rows))
        table = jnp.concatenate(rows, axis=0)
        col = jnp.sum(table, axis=1, keepdims=True)
        spread = jnp.where(iota((16, 128), 0) == iota((16, 128), 1), col, 0.0)
        line = jnp.sum(spread, axis=0, keepdims=True)
        nodes = (counts_ref[0, 0] + counts_ref[0, 1]).astype(F32)
        stats_ref[...] = jnp.where(iota((1, 128), 1) == 15, nodes, line)


def exchange_kernel(nx, ny, total, proj_ref, stats_ref, halo_ref, gnorm_ref,
                    near, slot1, slot2, send1, recv1, send2, recv2, hs, hr):
    gx = lax.axis_index("gx")
    gy = lax.axis_index("gy")
    barrier = pltpu.get_barrier_semaphore()
    for d in range(1, ny):
        pl.semaphore_signal(barrier, inc=1, device_id=(gx, lax.rem(gy + d, ny)), device_id_type=MESH)
    for d in range(1, nx):
        pl.semaphore_signal(barrier, inc=1, device_id=(lax.rem(gx + d, nx), gy), device_id_type=MESH)
    pl.semaphore_wait(barrier, nx + ny - 2)

    slot1[0] = stats_ref[...]
    copies = []
    for d in range(1, ny):
        c = pltpu.make_async_remote_copy(
            src_ref=slot1.at[0], dst_ref=slot1.at[d], send_sem=send1.at[d], recv_sem=recv1.at[d],
            device_id=(gx, lax.rem(gy + d, ny)), device_id_type=MESH)
        c.start()
        copies.append(c)
    for c in copies:
        c.wait()
    part = [slot1[lax.rem(gy - n + ny, ny)] for n in range(ny)]
    line = part[0]
    for x in part[1:]:
        line = line + x
    slot2[0] = line
    copies = []
    for d in range(1, nx):
        c = pltpu.make_async_remote_copy(
            src_ref=slot2.at[0], dst_ref=slot2.at[d], send_sem=send2.at[d], recv_sem=recv2.at[d],
            device_id=(lax.rem(gx + d, nx), gy), device_id_type=MESH)
        c.start()
        copies.append(c)
    for c in copies:
        c.wait()
    part = [slot2[lax.rem(gx - n + nx, nx)] for n in range(nx)]
    line = part[0]
    for x in part[1:]:
        line = line + x

    lane = iota((1, 128), 1)

    def pick(n):
        return jnp.sum(jnp.where(lane == n, line, 0.0), axis=1, keepdims=True)

    nodes = pick(15)
    steps = proj_ref.shape[-1]
    inv = [1.0 / jnp.sqrt(pick(v) / (nodes * steps) + 1e-06) for v in range(NV)]
    g = jnp.zeros((1, 1), F32)
    for n, (a, b) in enumerate(PAIRS):
        g = g + (1.0 if a == b else 2.0) * pick(NV + n) * inv[a] * inv[b]
    gnorm_ref[...] = jnp.broadcast_to(g / (total * R * steps), (1, 128))
    for s in range(2):
        x = proj_ref[s, 0] * inv[0]
        for v in range(1, NV):
            x = x + proj_ref[s, v] * inv[v]
        near[1, 1 + s] = x
    up, down = lax.rem(gx + 1, nx), lax.rem(gx + nx - 1, nx)
    right, left = lax.rem(gy + 1, ny), lax.rem(gy + ny - 1, ny)

    def send(n, src, dst, dev):
        return pltpu.make_async_remote_copy(
            src_ref=src, dst_ref=dst, send_sem=hs.at[n], recv_sem=hr.at[n], device_id=dev, device_id_type=MESH)

    own = near.at[1, pl.ds(1, 2)]
    one = send(0, own, near.at[0, pl.ds(1, 2)], (up, gy))
    two = send(1, own, near.at[2, pl.ds(1, 2)], (down, gy))
    one.start()
    two.start()
    one.wait()
    two.wait()
    three = send(2, near.at[:, 2], near.at[:, 0], (gx, right))
    four = send(3, near.at[:, 1], near.at[:, 3], (gx, left))
    three.start()
    four.start()
    three.wait()
    four.wait()
    halo_ref[...] = near[...]


def invert_block(x_ref, panels):
    lane = iota((8, 128), 1)
    sub = iota((8, 128), 0)
    inner = lane % HALF
    half = lane - inner

    def panel(p, carry):
        off = p * 8
        xs = [x_ref[8 * i:8 * i + 8, :] for i in range(panels)]
        rb = x_ref[pl.ds(pl.multiple_of(off, 8), 8), :]
        idx = [half + off + l for l in range(8)]
        c = [jnp.take_along_axis(rb, idx[l], axis=1) for l in range(8)]
        for k in range(8):
            r = 1.0 / jnp.broadcast_to(c[k][k:k + 1, :], (8, 128))
            f = jnp.where(sub == k, -r, c[k] * r)
            new = []
            for j in range(8):
                if j == k:
                    new.append(-f)
                else:
                    t = jnp.broadcast_to(c[j][k:k + 1, :], (8, 128))
                    new.append(jnp.where(sub == k, 0.0, c[j]) - f * t)
            c = new
        inp = (inner >= off) & (inner < off + 8)
        rb = jnp.where(inp, jnp.where(inner - off == sub, 1.0, 0.0), rb)
        prods = [c[l] * jnp.broadcast_to(rb[l:l + 1, :], (8, 128)) for l in range(8)]
        while len(prods) > 1:
            prods = [prods[i] + prods[i + 1] for i in range(0, len(prods), 2)]
        q = prods[0]
        qb = [jnp.broadcast_to(q[l:l + 1, :], (8, 128)) for l in range(8)]
        for i in range(panels):
            prods = [jnp.take_along_axis(xs[i], idx[l], axis=1) * qb[l] for l in range(8)]
            while len(prods) > 1:
                prods = [prods[n] + prods[n + 1] for n in range(0, len(prods), 2)]
            x_ref[8 * i:8 * i + 8, :] = jnp.where(inp, 0.0, xs[i]) - prods[0]
        x_ref[pl.ds(pl.multiple_of(off, 8), 8), :] = q
        return carry

    lax.fori_loop(0, panels, panel, 0)


def fit_kernel(gy_size, grid_cols, adj_ref, halo_ref, gnorm_ref, op_ref, st_ref,
               hi_ref, lo_ref, a_ref, x_ref, y_ref):
    gx = lax.axis_index("gx")
    gy = lax.axis_index("gy")
    g = gnorm_ref[0:1, 0:1]
    rg = 1.0 / jnp.sqrt(g)
    steps = halo_ref.shape[-1]
    keep = iota((8, steps), 1) < steps - 1
    sub = iota((8, steps), 0)
    for s in range(2):
        own = halo_ref[1, 1 + s]
        st_ref[s] = own
        t = own * rg
        future = pltpu.roll(t, steps - 1, axis=1)
        tile = [jnp.where(keep, t[8 * a:8 * a + 8], 0.0) for a in range(3)]

        def put(n, x):
            hi, lo = split2(x)
            hi_ref[s, 8 * n:8 * n + x.shape[0], :] = hi
            lo_ref[s, 8 * n:8 * n + x.shape[0], :] = lo

        def turned(x, r):
            return pltpu.roll(x, 8 - r, axis=0) if r else x

        tiles = []
        for a in range(3):
            for r in range(4):
                tiles.append(tile[a] * turned(tile[a], r))
        for a, b in ((0, 1), (0, 2), (1, 2)):
            for r in range(8):
                tiles.append(tile[a] * turned(tile[b], r))
        opp = [tile[a] * turned(tile[a], 4) for a in range(3)]
        tiles.append(jnp.where(sub < 4, opp[0], opp[1]))
        one = jnp.where((sub == 4) & keep, jnp.broadcast_to(rg, (8, steps)), 0.0)
        tiles.append(jnp.where(sub < 4, opp[2], one))
        tiles += tile
        for b in range(3):
            node = adj_ref[0, s, b]
            row = node // grid_cols - gx + 1
            col = node % grid_cols - gy * 2 + 1
            x = halo_ref[row, col] * rg
            for a in range(3):
                tiles.append(jnp.where(keep, x[8 * a:8 * a + 8], 0.0))
        tiles += [future[8 * a:8 * a + 8] for a in range(3)]
        tiles.append(jnp.zeros((8, steps), F32))
        for n in range(0, len(tiles), 2):
            put(n, jnp.concatenate(tiles[n:n + 2], axis=0))
        top = 8 * len(tiles)
        hi_ref[s, top:512, :] = jnp.zeros((512 - top, steps), BF16)
        lo_ref[s, top:512, :] = jnp.zeros((512 - top, steps), BF16)

        for n in range(2):
            cols = slice(256 * n, 256 * n + 256)
            x = (mm_nt(hi_ref[s, 0:ROWS, :], hi_ref[s, cols, :])
                 + mm_nt(lo_ref[s, 0:ROWS, :], hi_ref[s, cols, :])
                 + mm_nt(hi_ref[s, 0:ROWS, :], lo_ref[s, cols, :]))
            diag = iota((ROWS, 256), 0) == iota((ROWS, 256), 1) + 256 * n
            a_ref[s, :, cols] = x + jnp.where(diag, 0.5 * steps, 0.0)

    lane = iota((8, 128), 1)
    for k in range(7):
        top = HALF * k
        size = min(HALF, ROWS - top)
        tile = k // 2
        odd = k % 2
        start = 128 * ((k + 1) // 2)
        rows = slice(top, top + size)
        left = lane[0:1] < HALF
        xa = a_ref[0, rows, 128 * tile:128 * tile + 128]
        xb = a_ref[1, rows, 128 * tile:128 * tile + 128]
        if odd:
            xa = pltpu.roll(xa, HALF, axis=1)
        else:
            xb = pltpu.roll(xb, HALF, axis=1)
        x_ref[0:size, :] = jnp.where(left, xa, xb)
        invert_block(x_ref, size // 8)
        xh, xl = split2(x_ref[0:size, :])
        for s in range(2):
            bh, bl = split2(a_ref[s, rows, start:512])
            zero = jnp.zeros((HALF, 512 - start), BF16)
            fill = jnp.zeros((HALF - size, 512 - start), BF16)

            def stack(b, second):
                parts = [b] if size == HALF else [b, fill]
                return jnp.concatenate([zero] + parts if second else parts + [zero], axis=0)

            bh, bl = stack(bh, s == 1), stack(bl, s == 1)
            w = mm(xh, bh) + mm(xl, bh) + mm(xh, bl)
            wh, wl = split2(w)
            wh, wl = stack(wh, odd), stack(wl, odd)
            ch, cl = split2(a_ref[s, :, 128 * tile:128 * tile + 128])
            a_ref[s, :, start:512] -= mm(ch, wh) + mm(cl, wh) + mm(ch, wl)
            a_ref[s, rows, start:512] = w

    for s in range(2):
        y = pltpu.roll(a_ref[s, :, 384:512], 128 - (ROWS - 384), axis=1)
        quad = iota((ROWS, 128), 0) < QUAD_END
        y_ref[...] = jnp.where(quad, y * rg, y)
        for n, m in enumerate(SOURCE):
            op_ref[s, n:n + 1, :] = y_ref[m:m + 1, 0:R]


def scan_call(snapshots, basis, counts):
    _, subs, nv, slots, steps = snapshots.shape
    return pl.pallas_call(
        scan_kernel,
        grid=(subs, nv),
        in_specs=[
            pl.BlockSpec(memory_space=pltpu.SMEM),
            pl.BlockSpec((None, None, None, slots, steps), lambda s, v: (0, s, v, 0, 0)),
            pl.BlockSpec((None, None, None, R, slots), lambda s, v: (0, s, v, 0, 0)),
        ],
        out_specs=[
            pl.BlockSpec((None, nv, R, steps), lambda s, v: (s, 0, 0, 0)),
            pl.BlockSpec((1, 128), lambda s, v: (0, 0)),
        ],
        out_shape=[
            jax.ShapeDtypeStruct((subs, nv, R, steps), F32),
            jax.ShapeDtypeStruct((1, 128), F32),
        ],
        scratch_shapes=[pltpu.VMEM((16, 8, 128), F32)],
        compiler_params=pltpu.CompilerParams(dimension_semantics=("arbitrary", "arbitrary")),
        name="scan",
    )(counts, snapshots, basis)


def exchange_call(proj, stats, nx, ny, total):
    steps = proj.shape[-1]
    vm = pl.BlockSpec(memory_space=pltpu.VMEM)
    dma = pltpu.SemaphoreType.DMA
    return pl.pallas_call(
        functools.partial(exchange_kernel, nx, ny, total),
        in_specs=[vm, vm],
        out_specs=[vm, vm],
        out_shape=[
            jax.ShapeDtypeStruct((3, 4, R, steps), F32),
            jax.ShapeDtypeStruct((1, 128), F32),
        ],
        scratch_shapes=[
            pltpu.VMEM((3, 4, R, steps), F32),
            pltpu.VMEM((ny, 1, 128), F32),
            pltpu.VMEM((nx, 1, 128), F32),
            dma((ny,)), dma((ny,)), dma((nx,)), dma((nx,)), dma((4,)), dma((4,)),
        ],
        compiler_params=pltpu.CompilerParams(collective_id=0, has_side_effects=True),
        name="exchange",
    )(proj, stats)


def fit_call(adj, halo, gnorm, ny):
    steps = halo.shape[-1]
    vm = pl.BlockSpec(memory_space=pltpu.VMEM)
    return pl.pallas_call(
        functools.partial(fit_kernel, ny, 2 * ny),
        in_specs=[pl.BlockSpec(memory_space=pltpu.SMEM), vm, vm],
        out_specs=[vm, vm],
        out_shape=[
            jax.ShapeDtypeStruct((2, 397, R), F32),
            jax.ShapeDtypeStruct((2, R, steps), F32),
        ],
        scratch_shapes=[
            pltpu.VMEM((2, 512, steps), BF16),
            pltpu.VMEM((2, 512, steps), BF16),
            pltpu.VMEM((2, ROWS, 512), F32),
            pltpu.VMEM((HALF, 128), F32),
            pltpu.VMEM((ROWS, 128), F32),
        ],
        name="fit",
    )(adj, halo, gnorm)


def solution(mesh):
    nx, ny = mesh.shape["gx"], mesh.shape["gy"]

    def body(snapshots, basis, counts, adj):
        proj, stats = scan_call(snapshots, basis, counts)
        total = nx * ny * snapshots.shape[1]
        halo, gnorm = exchange_call(proj, stats, nx, ny, total)
        op, st = fit_call(adj, halo, gnorm, ny)
        return op[None], st[None]

    lead = P("gx", "gy")
    return jax.shard_map(
        body,
        mesh=mesh,
        in_specs=(lead, lead, lead, lead),
        out_specs=(lead, lead),
        check_vma=False,
    )
```

time: 338 us -> 68.5 us (0.20); the launches traced: 333 us -> 68.1 us
  other arithmetic: 236 us -> 0 us
  Pallas kernels: 0 us -> 65.7 us
  blocking collectives: 39 us -> 0 us
  local copies, waits for them, and re-layouts: 21.6 us -> 1.82 us
  matrix products: 19.6 us -> 0 us
  starting transfers between devices: 9.79 us -> 0 us
  between operations: 4.41 us -> 0.64 us
    another operation x26 -> x0, other arithmetic: 217 us -> none  [the longest x18 134 us: solve_one(): factor = jnp.linalg.cholesky(gram)]
    pallas_call x0 -> x3, Pallas kernels: none -> 65.7 us  [the longest x1 28.2 us: exchange_call(): pl.pallas_call(functools.partial(exchange_kernel, nx, ny, total), in_spec...]
    psum x4 -> x0, blocking collectives: 39 us -> none  [one_axis_at_a_time(): x = lax.psum(x, axis)]
    dot_general x5 -> x0, matrix products: 10.4 us -> none  [the longest x1 3.43 us: body(): jnp.einsum('svrp,svpk->svrk', masked, values, preferred_element_type=jnp....]
    ppermute x4 -> x0, starting transfers between devices: 9.79 us -> none  [the longest x2 6.03 us: padded_2(): lax.ppermute(tail, axis, [(i, (i + 1) % count) for i in range(ends)])]
    another operation x20 -> x0, matrix products: 9.23 us -> none  [the longest x6 5.45 us: solve_one(): factor = jnp.linalg.cholesky(gram)]
    another operation x17 -> x0, local copies, waits for them, and re-layouts: 8.23 us -> none
    concatenate x1 -> x0, local copies, waits for them, and re-layouts: 8.01 us -> none  [build_features(): return jnp.concatenate(pieces, axis=1)]
  transfers between devices with their start and end apart: 4 -> 0, of which waited for: 1 -> 0; matrix products, arithmetic and copies ran while one was open for 3% -> 0% of each run, Pallas kernels for 0% -> 0%
where the time goes in v1:
time: 68.5 us; the launch traced here: 68.1 us
  Pallas kernels  65.7 us (96%)
  local copies, waits for them, and re-layouts  1.82 us (3%)
    pallas_call x1, Pallas kernels, exchange_call(): pl.pallas_call(functools.partial(exchange_kernel, nx, ny, total), in_spec...  28.2 us
    pallas_call x1, Pallas kernels, fit_call(): pl.pallas_call(functools.partial(fit_kernel, ny, 2 * ny), in_specs=[pl.Bl...  23.6 us
    pallas_call x1, Pallas kernels, scan_call(): pl.pallas_call(scan_kernel, grid=(subs, nv), in_specs=[pl.BlockSpec(memor...  13.8 us
    unnamed x1, local copies, waits for them, and re-layouts  1.82 us

profile of v1, /device:TPU:1, one launch (start us, length us, event | category | flops | bytes accessed | tf_op | source)
XLA Modules:
  0.0 68.1 jit_solution(16736965289422400961)
XLA Ops:
  0.6 13.8 %scan.1 = (f32[2,4,24,512]{3,2,1,0:T(8,128)}, f32[1,128]{1,0:T(1,128)}) custom-call(s32[1,2]{1,0:T(1,128)} %counts_ref.1, bf16[1,2,4,2048,512]{4,3,2,1,0:T(8,128)(2,1)} %vals_ref.1, bf16[1,2,4,24,2048]{4,3,2,1,0:T(8,128)(2,1)} %modes_ref.1), custom_call_target="tpu_custom_call" | custom-call | tf_op jit(solution)/shard_map/scan/pallas_call | solution.py:336
  14.5 28.2 %exchange.1 = (f32[3,4,24,512]{3,2,1,0:T(8,128)}, f32[1,128]{1,0:T(1,128)}) custom-call(f32[2,4,24,512]{3,2,1,0:T(8,128)} %get-tuple-element.8.proj_ref, f32[1,128]{1,0:T(1,128)} %get-tuple-element.9.stats_ref), custom_call_target="tpu_custom_call" | custom-call | tf_op jit(solution)/shard_map/exchange/pallas_call | solution.py:362
  42.7 23.6 %fit.1 = (f32[2,397,24]{2,1,0:T(8,128)}, f32[2,24,512]{2,1,0:T(8,128)}) custom-call(s32[1,2,3]{2,1,0:T(2,128)} %adj_ref.1, f32[3,4,24,512]{3,2,1,0:T(8,128)} %get-tuple-element.10.halo_ref, f32[1,128]{1,0:T(1,128)} %get-tuple-element.11.gnorm_ref), custom_call_target="tpu_custom_call" | custom-call | tf_op jit(solution)/shard_map/fit/pallas_call | solution.py:384
  66.3 1.8 %copy.6 = f32[1,2,397,24]{2,3,1,0:T(8,128)} copy(f32[1,2,397,24]{3,2,1,0:T(8,128)} %bitcast.2) | data formatting | bytes 152448
